TPU v7x, 32 devices: a whole 2x2x4 slice. The times are simulated.
32 devices in a mesh: wall: 8 (over z, x), spec: 4 (over y, core).
Axes of the slice: x: 2, y: 2, z: 4, core: 2. Of those that a mesh axis runs over, the one named last changes fastest.
Arguments:
- signal: bfloat16 [4, 2, 256, 32, 10240], P(None, None, 'wall', None, 'spec'), may hold values from -6 to 6
- kx_index: int32 [128], replicated, may hold values from 0 to 5119
- kz_index: int32 [128], replicated, may hold values from 0 to 3
Outputs:
- phi: float32 [2, 128, 256, 256], P(None, 'spec', 'wall')
Inputs may be any that keep to these rules, and one draw needn't show every extreme that they name: `kx_index`: pairs may repeat.
All inputs are finite; a program needn't handle non-finite values.
Results may differ from a plain program's by a relative error of at most 0.0042.
Values sent between devices are 32-bit elements; how exact they have to be, the bound alone decides.
A program may use at most 128 MiB of HBM per device.

v0:
```python
import math

import jax
import jax.numpy as jnp
from jax import lax
from jax.sharding import PartitionSpec as P

NXW = 10240


def tables(kx_values, positions):
    phase = kx_values[:, None] * positions[None, :] % NXW
    angle = 2.0 * math.pi / NXW * phase.astype(jnp.float32)
    factor = float(NXW) ** (-0.5)
    return (
        (jnp.cos(angle) * factor).astype(jnp.bfloat16),
        (jnp.sin(angle) * factor).astype(jnp.bfloat16),
    )


def gram(left, right):
    high = lax.Precision.HIGHEST
    left_re, left_im = (left[:, 0], left[:, 1])
    right_re, right_im = (right[:, 0], right[:, 1])
    snaps = left.shape[3]
    real = (
        jnp.einsum("kys,kzs->kyz", left_re, right_re, precision=high)
        + jnp.einsum("kys,kzs->kyz", left_im, right_im, precision=high)
    ) / snaps
    imag = (
        jnp.einsum("kys,kzs->kyz", left_im, right_re, precision=high)
        - jnp.einsum("kys,kzs->kyz", left_re, right_im, precision=high)
    ) / snaps
    return jnp.stack([real, imag])


def on_device(signal, kx_index, kz_index):
    modes, parts, planes, snaps, width = signal.shape
    flat = signal.reshape(modes, parts, planes * snaps, width)
    positions = lax.axis_index("spec") * width + jnp.arange(width, dtype=jnp.int32)
    local_pairs = kx_index.shape[0] // lax.axis_size("spec")
    cosine, sine = tables(kx_index, positions)
    basis = jnp.stack([cosine, sine])
    grid = jnp.einsum("jcrx,bkx->cbjrk", flat, basis, preferred_element_type=jnp.float32)
    real = grid[0, 0] + grid[1, 1]
    imag = grid[1, 0] - grid[0, 1]
    onehot = (kz_index[None, :] == jnp.arange(modes, dtype=jnp.int32)[:, None]).astype(jnp.float32)
    high = lax.Precision.HIGHEST
    real_pick = jnp.einsum("jrk,jk->kr", real, onehot, precision=high)
    imag_pick = jnp.einsum("jrk,jk->kr", imag, onehot, precision=high)
    local = lax.psum_scatter(
        jnp.stack([real_pick, imag_pick], 1), "spec", scatter_dimension=0, tiled=True
    )
    spectra = local.reshape(local_pairs, 2, planes, snaps)
    return gram(spectra, lax.all_gather(spectra, "wall", axis=2, tiled=True))


def solution(mesh):
    return jax.shard_map(
        on_device,
        mesh=mesh,
        in_specs=(P(None, None, "wall", None, "spec"), P(), P()),
        out_specs=P(None, "spec", "wall", None),
        check_vma=False,
    )
```

profile of v0, /device:TPU:0, one launch (start us, length us, event | category | flops | bytes accessed | tf_op | source)
XLA Modules:
  0.0 232.7 jit_solution(1321455280911562527)
XLA Ops:
  6.5 0.0 reduce-scatter.2.cloned.1.call-start
  6.5 0.7 fusion.23
  7.2 0.2 copy.14
  7.4 6.4 %multiply_convert_fusion.1 = (bf16[1,128,2560]{2,1,0:T(8,128)(2,1)S(1)}, bf16[1,128,2560]{2,1,0:T(8,128)(2,1)S(1)}) fusion(s32[2560]{0:T(1024)S(1)} %iota_add_fusion, s32[128]{0:T(128)} %param.4), kind=kLoop, calls=%fused_computation.23 | loop fusion | flops 4259840 | bytes 1321472 | tf_op jit(solution)/shard_map/convert_element_type | solution.py:16
  13.8 21.9 %convolution_bitcast_fusion = f32[2,2,4,1024,128]{3,4,0,2,1:T(8,128)} fusion(bf16[4,2,1024,2560,1]{3,2,1,0,4:T(8,128)(2,1)} %bitcast.45, bf16[1,128,2560]{2,1,0:T(8,128)(2,1)S(1)} %get-tuple-element.10, bf16[1,128,2560]{2,1,0:T(8,128)(2,1)S(1)} %get-tuple-element.9), kind=kOutput, calls=%fused_computation | convolution fusion | flops 10740039680 | bytes 51642368 | tf_op jit(solution)/shard_map/jcrx,bkx->cbjrk/dot_general | solution.py:44
  35.7 4.4 %fusion.1 = (f32[4,1024,128]{1,2,0:T(8,128)S(1)}, f32[4,1024,128]{1,2,0:T(8,128)S(1)}) fusion(f32[2,2,4,1024,128]{3,4,0,2,1:T(8,128)} %convolution_bitcast_fusion), kind=kLoop, calls=%fused_computation.4 | loop fusion | flops 1048576 | bytes 12582912 | tf_op jit(solution)/shard_map/add | solution.py:45
  40.1 3.3 %fusion.4 = f32[128,1,1024]{2,1,0:T(1,128)S(1)} fusion(pred[4,128,1]{0,2,1:T(4,128)(4,1)S(1)} %copy.14, f32[4,1024,128]{1,2,0:T(8,128)S(1)} %get-tuple-element.7), kind=kOutput, calls=%fused_computation.8 | convolution fusion | flops 6291456 | bytes 2621952 | tf_op jit(solution)/shard_map/jrk,jk->kr/dot_general | solution.py:49
  43.5 3.3 %fusion.2 = f32[128,1,1024]{2,1,0:T(1,128)S(1)} fusion(pred[4,128,1]{0,2,1:T(4,128)(4,1)S(1)} %copy.14, f32[4,1024,128]{1,2,0:T(8,128)S(1)} %get-tuple-element.8), kind=kOutput, calls=%fused_computation.6 | convolution fusion | flops 6291456 | bytes 2621952 | tf_op jit(solution)/shard_map/jrk,jk->kr/dot_general | solution.py:50
  46.8 0.1 copy.17
  46.9 0.1 copy.15
  47.0 1.1 pad_maximum_fusion.1
  48.1 0.0 reduce-scatter.2.cloned.1.call-update
  48.1 0.0 all-gather.2.cloned.1.call-start
  48.2 27.6 %reduce-scatter.2.cloned.1.call-done = f32[32,2,1024]{2,0,1:T(8,128)} async-done(((f32[128,2,1024]{2,0,1:T(8,128)}), f32[32,2,1024]{2,0,1:T(8,128)}) %reduce-scatter.2.cloned.1.call-update) | async-done | bytes 262160 | tf_op jit(solution)/shard_map/reduce_scatter | solution.py:51
  75.8 1.3 reshape.135
  77.1 1.6 copy.9
  78.7 0.0 all-gather.2.cloned.1.call-update
  78.7 124.6 %all-gather.2.cloned.1.call-done = f32[32,2,256,32]{3,0,1,2:T(8,128)} async-done(((f32[32,2,32,32]{3,0,1,2:T(8,128)}), f32[32,2,256,32]{3,0,1,2:T(8,128)}) %all-gather.2.cloned.1.call-update) | async-done | bytes 2097168 | tf_op jit(solution)/shard_map/all_gather | solution.py:55
  203.3 7.7 %fusion.25 = (f32[32,1,256,32]{3,0,1,2:T(8,128)}, f32[32,1,256,32]{3,0,1,2:T(8,128)}) fusion(f32[32,2,256,32]{3,0,1,2:T(8,128)} %all-gather.2.cloned.1.call-done), kind=kLoop, calls=%fused_computation.41 | loop fusion | bytes 4194304 | tf_op jit(solution)/shard_map/slice | solution.py:24
  211.0 3.5 %copy.18 = f32[32,1,256,32]{2,3,0,1:T(8,128)S(1)} copy(f32[32,1,256,32]{3,0,1,2:T(8,128)} %get-tuple-element.6) | data formatting | bytes 2097152
  214.6 1.0 fusion.19
  215.6 2.0 fusion.21
  217.6 3.5 %copy.19 = f32[32,1,256,32]{2,3,0,1:T(8,128)S(1)} copy(f32[32,1,256,32]{3,0,1,2:T(8,128)} %get-tuple-element.5) | data formatting | bytes 2097152
  221.1 2.3 fusion.9
  223.3 1.1 fusion.7
  224.4 1.5 pad_maximum_fusion
  (1 shorter events, 0.0 us)
Async XLA Ops:
  6.5 69.3 %reduce-scatter.2.cloned.1.call-start = ((), (), s32[]{:S(2)}) async-start(), calls=%async_computation.1 | async-start | bytes 1310720 | tf_op jit(solution)/shard_map/reduce_scatter | solution.py:51
  48.1 155.2 %all-gather.2.cloned.1.call-start = ((), (), s32[]{:S(2)}) async-start(), calls=%async_computation.2 | async-start | bytes 9437184 | tf_op jit(solution)/shard_map/all_gather | solution.py:55
Sparse Core Ops, SparseCore 0:
  48.3 27.4 reduce-scatter.1
  78.8 124.4 all-gather.1
where the time goes:
time: 233 us
  waiting for transfers between devices  152 us (65%)
  matrix products  34.9 us (15%)
  local copies, waits for them, and re-layouts  18 us (8%)
  other arithmetic  14 us (6%)
  between operations  13.5 us (6%)
    all_gather x1, waiting for transfers between devices, on_device(): return gram(spectra, lax.all_gather(spectra, 'wall', axis=2, tiled=True))  125 us
    reduce_scatter x1, waiting for transfers between devices, on_device(): lax.psum_scatter(jnp.stack([real_pick, imag_pick], 1), 'spec', scatter_di...  27.6 us
    dot_general x1, matrix products, on_device(): jnp.einsum('jcrx,bkx->cbjrk', flat, basis, preferred_element_type=jnp.flo...  21.9 us
    slice x1, local copies, waits for them, and re-layouts, gram(): right_re, right_im = (right[:, 0], right[:, 1])  7.72 us
    unnamed x2, local copies, waits for them, and re-layouts  7.02 us
    convert_element_type x1, other arithmetic, tables(): (jnp.cos(angle) * factor).astype(jnp.bfloat16)  6.42 us
  transfers between devices with their start and end apart: 2, of which 2 were waited for; matrix products, arithmetic and copies ran while one was open for 0% of the time, Pallas kernels for 0%

commit v1 on v0

v1 whole, which is shorter than its diff:
```python
import functools
import math

import jax
import jax.numpy as jnp
from jax import lax
from jax.experimental import pallas as pl
from jax.experimental.pallas import tpu as pltpu
from jax.sharding import PartitionSpec as P

LANES = 128
ROWS = 256
VMEM_BYTES = 66_000_000


def angle_tables(kx_index, kz_index, modes, width, shards, me):
    total = width * shards
    pairs = kx_index.shape[0]
    kk = pairs // shards // 2

    def columns(v):
        v = jnp.broadcast_to(v.reshape(shards, 2, 1, kk), (shards, 2, 2, kk))
        return v.reshape(1, 2 * pairs)

    kx, kz = columns(kx_index), columns(kz_index)
    shift = jnp.broadcast_to(jnp.arange(2, dtype=jnp.int32).reshape(1, 1, 2, 1) * (total // 4), (shards, 2, 2, kk)).reshape(1, 2 * pairs)
    step = 2.0 * math.pi / total
    low = ((kx * jnp.arange(LANES, dtype=jnp.int32)[:, None] + shift) % total).astype(jnp.float32) * step
    at = me * width + LANES * jnp.arange(width // LANES, dtype=jnp.int32)
    high = ((kx * at[:, None]) % total).astype(jnp.float32) * step
    factor = float(total) ** -0.5
    c, s = jnp.cos(low) * factor, jnp.sin(low) * factor
    base = jnp.stack([jnp.stack([c, s]), jnp.stack([-s, c])], 1)
    mask = (kz == jnp.arange(modes, dtype=jnp.int32)[:, None]).astype(jnp.float32)[:, None, None, :]
    turn = jnp.stack([jnp.cos(high), jnp.sin(high)], 1)[None] * mask
    return base, turn


def transform_kernel(chunks, jcs, hs, base, turn, signal, out, xbuf, bbuf, acc, sems):
    def copy(y, q):
        return pltpu.make_async_copy(signal.at[q, pl.ds(y * ROWS, ROWS)], xbuf.at[y, q], sems.at[y, q])

    for y in range(chunks):
        @pl.loop(0, jcs)
        def _(q):
            copy(y, q).start()

    @pl.loop(0, jcs)
    def _(q):
        j, c = q // 2, q % 2

        @pl.loop(0, hs)
        def _(h):
            t = turn[j, h]
            v = base[c, 0] * t[0:1] + base[c, 1] * t[1:2]
            bbuf[q, pl.ds(pl.multiple_of(h * LANES, LANES), LANES)] = v.astype(jnp.bfloat16)

    for y in range(chunks):
        acc[...] = jnp.zeros_like(acc)

        @pl.loop(0, jcs)
        def _(q):
            copy(y, q).wait()
            acc[...] += jnp.dot(xbuf[y, q], bbuf[q], preferred_element_type=jnp.float32)

        out[:, y * ROWS:(y + 1) * ROWS] = acc[...].T


def gram_kernel(per, snaps, own, full, out):
    lane = lax.broadcasted_iota(jnp.int32, (1, LANES), 1)
    first = lane < LANES // 2
    is_re = (lane % (2 * snaps)) < snaps
    for i in range(per):
        mine = own[:, i, :] * (1.0 / snaps)
        right = full[:, i, :].astype(jnp.bfloat16)
        swap = jnp.where(is_re, pltpu.roll(mine, LANES - snaps, 1), -pltpu.roll(mine, snaps, 1))
        zero = jnp.zeros_like(mine)
        left = jnp.concatenate([jnp.where(first, mine, zero), jnp.where(first, zero, mine),
                                jnp.where(first, swap, zero), jnp.where(first, zero, swap)], 0)
        hi = left.astype(jnp.bfloat16)
        lo = (left - hi.astype(jnp.float32)).astype(jnp.bfloat16)
        dims = (((1,), (1,)), ((), ()))
        got = lax.dot_general(jnp.concatenate([hi, lo], 1), jnp.concatenate([right, right], 1), dims,
                              preferred_element_type=jnp.float32)
        out[:, :, i] = got.reshape(2, 2, mine.shape[0], full.shape[0])


def gram(own, full, snaps):
    planes, kk, _ = own.shape
    total = full.shape[0]
    per = kk if kk < 8 else 8
    return pl.pallas_call(
        functools.partial(gram_kernel, per, snaps),
        grid=(kk // per,),
        in_specs=[pl.BlockSpec((planes, per, LANES), lambda g: (0, g, 0)),
                  pl.BlockSpec((total, per, LANES), lambda g: (0, g, 0))],
        out_specs=pl.BlockSpec((2, 2, per, planes, total), lambda g: (0, 0, g, 0, 0)),
        out_shape=jax.ShapeDtypeStruct((2, 2, kk, planes, total), jnp.float32),
    )(own, full)


def on_device(signal, kx_index, kz_index):
    modes, parts, planes, snaps, width = signal.shape
    shards = lax.axis_size("spec")
    me = lax.axis_index("spec")
    pairs = kx_index.shape[0]
    kk = pairs // shards // 2
    jcs, rows, cols, hs = modes * parts, planes * snaps, 2 * pairs, width // LANES
    chunks = rows // ROWS
    base, turn = angle_tables(kx_index, kz_index, modes, width, shards, me)
    partial = pl.pallas_call(
        functools.partial(transform_kernel, chunks, jcs, hs),
        in_specs=[pl.BlockSpec(memory_space=pltpu.VMEM)] * 2 + [pl.BlockSpec(memory_space=pl.ANY)],
        out_specs=pl.BlockSpec(memory_space=pltpu.VMEM),
        out_shape=jax.ShapeDtypeStruct((cols, rows), jnp.float32),
        scratch_shapes=[
            pltpu.VMEM((chunks, jcs, ROWS, width), jnp.bfloat16),
            pltpu.VMEM((jcs, width, cols), jnp.bfloat16),
            pltpu.VMEM((ROWS, cols), jnp.float32),
            pltpu.SemaphoreType.DMA((chunks, jcs)),
        ],
        compiler_params=pltpu.CompilerParams(vmem_limit_bytes=VMEM_BYTES),
    )(base, turn, signal.reshape(jcs, rows, width))
    local = lax.psum_scatter(partial, "spec", scatter_dimension=0, tiled=True)
    own = local.reshape(2, 2, kk, planes, snaps).transpose(3, 2, 0, 1, 4).reshape(planes, kk, 4 * snaps)
    full = lax.all_gather(own, "wall", axis=0, tiled=True)
    out = gram(own, full, snaps)
    return out.reshape(2, 2 * kk, planes, full.shape[0])


def solution(mesh):
    return jax.shard_map(
        on_device,
        mesh=mesh,
        in_specs=(P(None, None, "wall", None, "spec"), P(), P()),
        out_specs=P(None, "spec", "wall", None),
        check_vma=False,
    )
```

time: 233 us -> 127 us (0.55)
  waiting for transfers between devices: 152 us -> 76.9 us
  matrix products: 34.9 us -> 0 us
  Pallas kernels: 0 us -> 27.7 us
  local copies, waits for them, and re-layouts: 18 us -> 5.46 us
  other arithmetic: 14 us -> 2.94 us
    all_gather x1, waiting for transfers between devices: 125 us -> 49.2 us  [on_device(): full = lax.all_gather(own, 'wall', axis=0, tiled=True)]
    dot_general x7 -> x0, matrix products: 34.9 us -> none  [the longest x1 21.9 us: on_device(): jnp.einsum('jcrx,bkx->cbjrk', flat, basis, preferred_element_type=jnp.flo...]
    pallas_call x0 -> x2, Pallas kernels: none -> 27.7 us  [the longest x1 22.7 us: on_device(): pl.pallas_call(functools.partial(transform_kernel, chunks, jcs, hs), in_s...]
    slice x1 -> x0, local copies, waits for them, and re-layouts: 7.72 us -> none  [gram(): right_re, right_im = (right[:, 0], right[:, 1])]
    unnamed x2 -> x0, local copies, waits for them, and re-layouts: 7.02 us -> none
    convert_element_type x1, other arithmetic: 6.42 us -> 0.01 us  [angle_tables(): (kz == jnp.arange(modes, dtype=jnp.int32)[:, None]).astype(jnp.float32)]
    add x2 -> x1, other arithmetic: 4.4 us -> 0.01 us  [angle_tables(): at = me * width + LANES * jnp.arange(width // LANES, dtype=jnp.int32)]
where the time goes in v1:
time: 127 us; the launch traced here: 126 us
  waiting for transfers between devices  76.9 us (61%)
  Pallas kernels  27.7 us (22%)
  between operations  13.5 us (11%)
  local copies, waits for them, and re-layouts  5.46 us (4%)
  other arithmetic  2.94 us (2%)
    all_gather x1, waiting for transfers between devices, on_device(): full = lax.all_gather(own, 'wall', axis=0, tiled=True)  49.2 us
    reduce_scatter x1, waiting for transfers between devices, on_device(): local = lax.psum_scatter(partial, 'spec', scatter_dimension=0, tiled=True)  27.6 us
    pallas_call x1, Pallas kernels, on_device(): pl.pallas_call(functools.partial(transform_kernel, chunks, jcs, hs), in_s...  22.7 us
    pallas_call x1, Pallas kernels, gram(): pl.pallas_call(functools.partial(gram_kernel, per, snaps), grid=(kk // pe...  4.99 us
    reshape x3, local copies, waits for them, and re-layouts, on_device(): local.reshape(2, 2, kk, planes, snaps).transpose(3, 2, 0, 1, 4)  3.63 us
  transfers between devices with their start and end apart: 2, of which 2 were waited for; matrix products, arithmetic and copies ran while one was open for 0% of the time, Pallas kernels for 0%

profile of v1, /device:TPU:0, one launch (start us, length us, event | category | flops | bytes accessed | tf_op | source)
XLA Modules:
  0.0 126.5 jit_solution(15691770612308136385)
XLA Ops:
  6.5 0.0 reduce-scatter.2.cloned.1.call-start
  6.5 0.7 broadcast_in_dim.10
  7.3 0.1 mul.147
  7.4 0.7 broadcast_in_dim.13
  8.1 0.1 eq.23
  8.2 0.1 broadcast_in_dim.12
  8.3 0.1 add.75
  8.4 0.7 fusion.10
  9.1 0.6 sine_multiply_fusion
  9.8 0.7 broadcast_multiply_fusion.turn
  10.5 0.8 pad_maximum_fusion.base
  11.3 22.7 %shard_map.37 = f32[256,1024]{1,0:T(8,128)} custom-call(f32[2,2,128,256]{3,2,1,0:T(8,128)} %pad_maximum_fusion.base, f32[4,20,2,256]{3,2,1,0:T(2,128)} %broadcast_multiply_fusion.turn, bf16[8,1024,2560]{2,1,0:T(8,128)(2,1)} %bitcast.11), custom_call_target="tpu_custom_call" | custom-call | tf_op jit(solution)/shard_map/pallas_call | solution.py:111
  34.0 0.0 reduce-scatter.2.cloned.1.call-update
  34.1 0.0 all-gather.2.cloned.1.call-start
  34.1 27.6 %reduce-scatter.2.cloned.1.call-done = f32[64,1024]{1,0:T(8,128)} async-done(((f32[256,1024]{1,0:T(8,128)}), f32[64,1024]{1,0:T(8,128)}) %reduce-scatter.2.cloned.1.call-update) | async-done | bytes 262160 | tf_op jit(solution)/shard_map/reduce_scatter | solution.py:124
  61.7 1.3 %reshape.381 = f32[2,2,16,32,32]{4,3,2,1,0:T(8,128)S(1)} reshape(f32[64,1024]{1,0:T(8,128)} %reduce-scatter.2.cloned.1.call-done) | data formatting | bytes 524288 | tf_op jit(solution)/shard_map/reshape | solution.py:125
  63.0 0.8 copy.9
  63.8 1.5 %reshape.382.own = f32[32,16,128]{2,1,0:T(8,128)} reshape(f32[32,16,2,2,32]{4,3,2,1,0:T(2,128)S(1)} %bitcast.12) | data formatting | bytes 524288 | tf_op jit(solution)/shard_map/reshape | solution.py:125
  65.4 0.0 all-gather.2.cloned.1.call-update
  65.4 49.2 %all-gather.2.cloned.1.call-done.full = f32[256,16,128]{2,1,0:T(8,128)} async-done(((f32[32,16,128]{2,1,0:T(8,128)}), f32[256,16,128]{2,1,0:T(8,128)}) %all-gather.2.cloned.1.call-update) | async-done | bytes 2097168 | tf_op jit(solution)/shard_map/all_gather | solution.py:126
  114.6 5.0 %shard_map.38 = f32[2,2,16,32,256]{4,3,2,1,0:T(8,128)} custom-call(f32[32,16,128]{2,1,0:T(8,128)} %reshape.382.own, f32[256,16,128]{2,1,0:T(8,128)} %all-gather.2.cloned.1.call-done.full), custom_call_target="tpu_custom_call" | custom-call | tf_op jit(solution)/shard_map/pallas_call | solution.py:92
  (7 shorter events, 0.1 us)
Async XLA Ops:
  6.5 55.2 %reduce-scatter.2.cloned.1.call-start = ((), (), s32[]{:S(2)}) async-start(), calls=%async_computation.1 | async-start | bytes 1310720 | tf_op jit(solution)/shard_map/reduce_scatter | solution.py:124
  34.1 80.6 %all-gather.2.cloned.1.call-start = ((), (), s32[]{:S(2)}) async-start(), calls=%async_computation.2 | async-start | bytes 2359296 | tf_op jit(solution)/shard_map/all_gather | solution.py:126
Sparse Core Ops, SparseCore 0:
  34.2 27.4 reduce-scatter.1
  65.5 49.0 all-gather.1
